TPU v7x, 256 devices: a whole 4x4x8 slice. The times are simulated.
256 devices in a mesh: grp: 8 (over z), bis: 32 (over x, y, core).
Axes of the slice: x: 4, y: 4, z: 8, core: 2. Of those that a mesh axis runs over, the one named last changes fastest.
Arguments:
- state: float32 [5, 32768, 512], P(None, ('grp', 'bis')), may hold values from -0.75 to 2, as said below
- order: int32 [256, 32], P(('grp', 'bis')), may hold values from 0 to 31, each once within a row
- sweep: float32 [32768, 512], P(('grp', 'bis')), may hold values from 0.1 to 0.45
- owner: int32 [8192, 1], P(('grp', 'bis')), may hold values from 0 to 31; in each aligned block of 32 rows (0 to 31, 32 to 63, ...) at most 2 rows name the same one
- slot_target: int32 [8192], P(('grp', 'bis')), may hold values from 0 to 31
Outputs:
- mass_out: float32 [32768, 512], P(('grp', 'bis'))
- energy_out: float32 [32768, 512], P(('grp', 'bis'))
- velocity: float32 [2, 32768, 512], P(None, ('grp', 'bis'))
Inputs may be any that keep to these rules, and one draw needn't show every extreme that they name: `state`: velocities up to 0.75 in size, densities and energies from 1 to 2, adiabatic indices from 1.3 to 1.7. `order`: each row of a device is a permutation. Among the row blocks of one device no owner is named more than 2 times, a bound that some block reaches.
All inputs are finite; a program needn't handle non-finite values.
Results may differ from a plain program's by a relative error of at most 0.00016.
Values sent between devices are 32-bit elements; how exact they have to be, the bound alone decides.
A program may use at most 64 MiB of HBM per device.

v0:
```python
import jax
import jax.numpy as jnp
from jax import lax
from jax.sharding import PartitionSpec as P

STEPS = 2
CAP = 2


STEP_DT = 0.15


def from_partner(block, axis, bit):
    count = lax.axis_size(axis)
    route = []
    for low in range(count):
        high = low | 1 << bit
        if high != low and high < count:
            route += [(low, high), (high, low)]
    return lax.ppermute(block, axis, route)


def with_halo(block, sides, width):
    for axis, dim in sides:
        count = lax.axis_size(axis)
        forward = [(i, i + 1) for i in range(count - 1)]
        backward = [(target, source) for source, target in forward]
        low = lax.ppermute(
            lax.slice_in_dim(block, block.shape[dim] - width, None, axis=dim), axis, forward
        )
        high = lax.ppermute(lax.slice_in_dim(block, 0, width, axis=dim), axis, backward)
        block = jnp.concatenate([low, block, high], axis=dim)
    return block


def advance(fields, volume, valid):
    rho = fields[0]
    ene = fields[1]
    velu = fields[2]
    velv = fields[3]
    gam = fields[4]
    press = (gam - 1.0) * rho * ene
    wide_p = jnp.pad(press[1:-1], ((0, 0), (1, 1)))
    wide_v = jnp.pad(velv[1:-1], ((0, 0), (1, 1)))
    grad_x = 0.5 * (press[2:] - press[:-2])
    grad_y = 0.5 * (wide_p[:, 2:] - wide_p[:, :-2])
    spread = 0.5 * (velu[2:] - velu[:-2] + wide_v[:, 2:] - wide_v[:, :-2])
    dens = jnp.where(valid, rho[1:-1], 1.0)
    growth = 1.0 + STEP_DT * spread
    center_g = gam[1:-1]
    updated = jnp.stack(
        [
            dens / growth,
            ene[1:-1] * (1.0 - STEP_DT * (center_g - 1.0) * spread),
            velu[1:-1] - STEP_DT * grad_x / dens,
            velv[1:-1] - STEP_DT * grad_y / dens,
            center_g,
        ]
    )
    updated = jnp.where(valid[None], updated, 0.0)
    return (updated, volume * growth)


def shards(state, order, sweep, owner, slot_target):
    rows = state.shape[1]
    width = state.shape[2]
    nbis = lax.axis_size("bis")
    block_rows = rows // nbis
    flat = block_rows * width
    picked = jnp.take(state.reshape(5, nbis, flat), order[0], axis=1)
    levels = nbis.bit_length() - 1
    bis_index = lax.axis_index("bis")
    moved = picked
    for level in range(levels):
        halves = moved.reshape(5, nbis >> level + 1, 2, 1 << level, flat)
        lower = halves[:, :, 0]
        upper = halves[:, :, 1]
        keep_low = bis_index >> level & 1 == 0
        outgoing = jnp.where(keep_low, upper, lower)
        incoming = from_partner(outgoing, "bis", level)
        lower = jnp.where(keep_low, lower, incoming)
        upper = jnp.where(keep_low, incoming, upper)
        moved = jnp.stack([lower, upper], axis=2).reshape(5, nbis, flat)
    fields = moved.reshape(5, rows, width)
    volume = jnp.ones((rows, width), jnp.float32)
    valid = jnp.ones((rows, 1), bool)
    for step in range(STEPS):
        padded = with_halo(fields, ((("grp", "bis"), 1),), 1)
        fields, volume = advance(padded, volume, valid)
    mass = fields[0] * volume
    heat = mass * fields[1]
    frac = sweep * volume / (1.0 + volume)
    amounts = jnp.stack([mass, heat])
    stay = ((1.0 - frac) * amounts).reshape(2, nbis, block_rows, width)
    leave = jnp.roll((frac * amounts).reshape(2, nbis, block_rows, width), 1, axis=2)
    partial_value = (stay + leave).reshape(2, nbis, flat)
    target = owner[:, 0]
    hits = (target[:, None] == jnp.arange(nbis, dtype=jnp.int32)[None, :]).astype(jnp.int32)
    rank = jnp.sum(jnp.cumsum(hits, axis=0) * hits, axis=1) - 1
    position = target * CAP + rank
    select = (position[None, :] == jnp.arange(nbis * CAP, dtype=jnp.int32)[:, None]).astype(
        jnp.float32
    )
    outgoing = jnp.einsum("pb,qbf->qpf", select, partial_value, precision=lax.Precision.HIGHEST)
    filled = jnp.sum(select, axis=1) > 0.0
    labels = jnp.where(
        filled,
        jnp.dot(select, slot_target.astype(jnp.float32), precision=lax.Precision.HIGHEST),
        -1.0,
    )
    arrived, arrived_labels = (
        lax.all_to_all(
            outgoing.reshape(2, nbis, CAP * flat), "bis", split_axis=1, concat_axis=1, tiled=True
        ),
        lax.all_to_all(
            labels.reshape(1, nbis, CAP), "bis", split_axis=1, concat_axis=1, tiled=True
        ),
    )
    arrived = arrived.reshape(2, nbis * CAP, flat)
    landing = (
        arrived_labels.reshape(nbis * CAP)[None, :] == jnp.arange(nbis, dtype=jnp.float32)[:, None]
    ).astype(jnp.float32)
    owned = jnp.einsum("bp,qpf->qbf", landing, arrived, precision=lax.Precision.HIGHEST).reshape(
        2, rows, width
    )
    return (owned[0], owned[1], fields[2:4])


def solution(mesh):
    placed = (
        P(None, ("grp", "bis"), None),
        P(("grp", "bis"), None),
        P(("grp", "bis"), None),
        P(("grp", "bis"), None),
        P(("grp", "bis")),
    )
    return jax.shard_map(
        shards,
        mesh=mesh,
        in_specs=placed,
        out_specs=(P(("grp", "bis"), None), P(("grp", "bis"), None), P(None, ("grp", "bis"), None)),
        check_vma=False,
    )
```

profile of v0, /device:TPU:1, one launch (start us, length us, event | category | flops | bytes accessed | tf_op | source)
XLA Modules:
  0.0 162.5 jit_solution(15025062032272084573)
XLA Ops:
  0.6 1.9 %reshape.203 = f32[5,32,2048]{2,1,0:T(8,128)S(1)} reshape(f32[5,128,512]{2,1,0:T(8,128)} %param.5) | data formatting | bytes 2621440 | tf_op jit(solution)/shard_map/reshape | solution.py:70
  2.5 0.8 copy.37
  3.4 0.5 broadcast.177
  3.9 0.7 reduce.6
  4.7 2.0 %gather_fusion = f32[32,5,2048]{2,1,0:T(8,128)} fusion(f32[5,32,2048]{2,0,1:T(8,128)S(1)} %copy.37, s32[1024]{0:T(1024)S(1)} %pad_clamp_fusion), kind=kCustom, calls=%fused_computation | custom fusion | bytes 2621568 | tf_op jit(solution)/shard_map/jit(_take)/gather | solution.py:70
  6.7 2.8 %copy_select_fusion = f32[5,16,2,1,2048]{4,2,3,1,0:T(2,128)S(1)} fusion(f32[5,16,2,1,2048]{4,0,2,1,3:T(8,128)} %bitcast.197, pred[16,2]{1,0:T(8,128)(4,1)S(1)} %compare_and_fusion), kind=kLoop, calls=%fused_computation.20 | loop fusion | flops 327680 | bytes 2621472 | tf_op jit(solution)/shard_map/jit(_take)/select_n | solution.py:70
  9.5 0.7 broadcast_select_fusion.2
  10.3 3.3 %collective-permute-start = (f32[5,16,1,2048]{3,2,1,0:T(1,128)S(1)}, f32[5,16,1,2048]{3,2,1,0:T(1,128)S(1)}, u32[]{:S(2)}, u32[]{:S(2)}) collective-permute-start(f32[5,16,1,2048]{3,2,1,0:T(1,128)S(1)} %broadcast_select_fusion.2), channel_id=1, source_target_pairs={{0,1},{1,0},{2,3},{3,2},{4,5},{5,4},{6,7},{7,6},{8,9},{9,8},{10,11... | collective-permute-start | bytes 1966088 | tf_op jit(solution)/shard_map/ppermute | solution.py:20
  13.5 1.7 %collective-permute-done = f32[5,16,1,2048]{3,2,1,0:T(1,128)S(1)} collective-permute-done((f32[5,16,1,2048]{3,2,1,0:T(1,128)S(1)}, f32[5,16,1,2048]{3,2,1,0:T(1,128)S(1)}, u32[]{:S(2)}, u32[]{:S(2)}) %collective-permute-start) | collective-permute-done | bytes 655392 | tf_op jit(solution)/shard_map/ppermute | solution.py:20
  15.3 1.1 broadcast_select_fusion.1
  16.4 1.1 broadcast_select_fusion.3
  17.5 0.3 collective-permute-start.1
  17.8 15.9 %collective-permute-done.1 = f32[5,8,2,2048]{3,2,1,0:T(2,128)S(1)} collective-permute-done((f32[5,8,2,2048]{3,2,1,0:T(2,128)S(1)}, f32[5,8,2,2048]{3,2,1,0:T(2,128)S(1)}, u32[]{:S(2)}, u32[]{:S(2)}) %collective-permute-start.1) | collective-permute-done | bytes 655392 | tf_op jit(solution)/shard_map/ppermute | solution.py:20
  33.7 1.3 select_bitcast_fusion.6
  35.0 0.7 pad_maximum_fusion.1
  35.7 0.8 copy.40
  36.5 0.8 reshape_reshape.13
  37.3 1.4 fusion.63
  38.7 0.5 bitcast_select_fusion.1
  39.2 1.3 collective-permute-start.2
  40.5 15.4 %collective-permute-done.2 = f32[5,4,4,2048]{3,1,2,0:T(4,128)S(1)} collective-permute-done((f32[5,4,4,2048]{3,1,2,0:T(4,128)S(1)}, f32[5,4,4,2048]{3,1,2,0:T(4,128)S(1)}, u32[]{:S(2)}, u32[]{:S(2)}) %collective-permute-start.2) | collective-permute-done | bytes 655392 | tf_op jit(solution)/shard_map/ppermute | solution.py:20
  55.9 0.6 select_bitcast_fusion.4
  56.5 0.6 pad_maximum_fusion.2
  57.1 0.8 copy.42
  58.0 0.5 reshape_reshape.14
  58.6 14.2 %collective-permute-done.3 = f32[5,2,8,2048]{3,2,1,0:T(8,128)S(1)} collective-permute-done((f32[5,2,8,2048]{3,2,1,0:T(8,128)S(1)}, f32[5,2,8,2048]{3,2,1,0:T(8,128)S(1)}, u32[]{:S(2)}, u32[]{:S(2)}) %collective-permute-start.3) | collective-permute-done | bytes 655392 | tf_op jit(solution)/shard_map/ppermute | solution.py:20
  73.1 1.1 collective-permute-start.4
  74.7 13.4 %collective-permute-done.4 = f32[5,1,16,2048]{3,2,0,1:T(8,128)S(1)} collective-permute-done((f32[5,1,16,2048]{3,2,0,1:T(8,128)S(1)}, f32[5,1,16,2048]{3,2,0,1:T(8,128)S(1)}, u32[]{:S(2)}, u32[]{:S(2)}) %collective-permute-start.4) | collective-permute-done | bytes 655392 | tf_op jit(solution)/shard_map/ppermute | solution.py:20
  88.3 1.2 copy.46
  89.5 1.6 %reshape_reshape.16 = f32[5,128,512]{2,1,0:T(8,128)S(1)} reshape(f32[5,1,2,16,2048]{4,3,2,0,1:T(8,128)} %copy.46) | data formatting | bytes 2621440 | tf_op jit(solution)/shard_map/reshape;reshape | solution.py:84
  91.2 5.7 %collective-permute-start.5 = (f32[5,1,512]{2,1,0:T(1,128)S(1)}, f32[5,1,512]{2,1,0:T(1,128)S(1)}, u32[]{:S(2)}, u32[]{:S(2)}) collective-permute-start(f32[5,1,512]{2,1,0:T(1,128)S(1)} %get-tuple-element.28), channel_id=1, source_target_pairs={{1,0},{2,1},{3,2},{4,3},{5,4},{6,5},{7,6},{8,7},{9,8},{10,9},{11,1... | collective-permute-start | bytes 30728 | tf_op jit(solution)/shard_map/ppermute | solution.py:31
  96.9 2.9 %collective-permute-start.6 = (f32[5,1,512]{2,1,0:T(1,128)S(1)}, f32[5,1,512]{2,1,0:T(1,128)S(1)}, u32[]{:S(2)}, u32[]{:S(2)}) collective-permute-start(f32[5,1,512]{2,1,0:T(1,128)S(1)} %get-tuple-element.29), channel_id=1, source_target_pairs={{0,1},{1,2},{2,3},{3,4},{4,5},{5,6},{6,7},{7,8},{8,9},{9,10},{10,1... | collective-permute-start | bytes 30728 | tf_op jit(solution)/shard_map/ppermute | solution.py:28
  99.8 0.9 fusion.31
  100.8 1.0 slice.242
  101.9 1.8 %slice.248 = f32[128,512]{1,0:T(8,128)} reshape(f32[1,1,2,16,2048]{4,3,0,2,1:T(8,128)} %get-tuple-element.25) | data formatting | bytes 524288 | tf_op jit(solution)/shard_map/slice | solution.py:54
  103.7 0.8 mul.116
  104.5 0.8 slice.251
  105.2 0.8 slice.261
  106.0 0.2 bitcast_dynamic-update-slice_fusion.3
  106.3 0.7 copy-done.4
  107.2 0.8 copy-done
  108.1 0.8 copy-done.3
  109.0 0.9 bitcast_dynamic-update-slice_fusion
  109.9 2.1 %collective-permute-start.7 = (f32[5,1,512]{2,1,0:T(1,128)S(1)}, f32[5,1,512]{2,1,0:T(1,128)S(1)}, u32[]{:S(2)}, u32[]{:S(2)}) collective-permute-start(f32[5,1,512]{2,1,0:T(1,128)S(1)} %get-tuple-element.20), channel_id=1, source_target_pairs={{1,0},{2,1},{3,2},{4,3},{5,4},{6,5},{7,6},{8,7},{9,8},{10,9},{11,1... | collective-permute-start | bytes 30728 | tf_op jit(solution)/shard_map/ppermute | solution.py:31
  112.0 3.6 %collective-permute-start.8 = (f32[5,1,512]{2,1,0:T(1,128)S(1)}, f32[5,1,512]{2,1,0:T(1,128)S(1)}, u32[]{:S(2)}, u32[]{:S(2)}) collective-permute-start(f32[5,1,512]{2,1,0:T(1,128)S(1)} %get-tuple-element.21), channel_id=1, source_target_pairs={{0,1},{1,2},{2,3},{3,4},{4,5},{5,6},{6,7},{7,8},{8,9},{9,10},{10,1... | collective-permute-start | bytes 30728 | tf_op jit(solution)/shard_map/ppermute | solution.py:28
  115.6 0.2 fusion
  115.8 0.7 reshape.206
  116.5 10.6 %all-to-all-start.1 = ((f32[1,32,2]{2,0,1:T(1,128)}), f32[1,32,2]{2,0,1:T(1,128)S(1)}, u32[]{:S(2)}, u32[]{:S(2)}) async-start(f32[1,32,2]{2,0,1:T(1,128)} %bitcast.37), calls=%async_computation.1 | async-start | bytes 32768 | tf_op jit(solution)/shard_map/all_to_all | solution.py:115
  127.3 2.6 %fusion.37 = (f32[1,128,512]{2,1,0:T(8,128)}, f32[1,128,512]{2,1,0:T(8,128)}, f32[128,512]{1,0:T(8,128)}, f32[128,512]{1,0:T(8,128)}, f32[128,512]{1,0:T(8,128)S(1)}) fusion(f32[128,512]{1,0:T(8,128)S(1)} %slice.246, f32[1,130,512]{2,1,0:T(8,128)S(1)} %fusion.11, f32[128,512]{1,0:T(8,128)S(1)} %get-tuple-element.9, f32[128,512]{1,0:T(8,128)S(1)} %copy-done.1, ...), kind=kLoop, calls=%fused_computation.102 | loop fusion | flops 1835008 | bytes 5263360 | tf_op jit(solution)/shard_map/stack | solution.py:51
  130.5 0.5 copy-done.9
  131.4 0.2 pad_maximum_fusion.5
  131.7 0.4 concatenate.35
  132.4 0.7 convolution_bitcast_fusion
  133.1 0.3 reshape.204
  133.4 1.8 %copy.47 = f32[2,32,4096]{2,0,1:T(2,128)} copy(f32[2,32,4096]{2,1,0:T(8,128)S(1)} %reshape.204) | data formatting | bytes 2097152 | tf_op jit(solution)/shard_map/reshape | solution.py:113
  135.2 7.5 %all-to-all-start = ((f32[2,32,4096]{2,0,1:T(2,128)}), f32[2,32,4096]{2,0,1:T(2,128)S(1)}, u32[]{:S(2)}, u32[]{:S(2)}) async-start(f32[2,32,4096]{2,0,1:T(2,128)} %copy.47), calls=%async_computation | async-start | bytes 2097152 | tf_op jit(solution)/shard_map/all_to_all | solution.py:112
  142.7 0.5 broadcast.178
  143.3 0.7 reduce.7
  144.1 0.8 pad_maximum_fusion.6
  144.9 14.7 %all-to-all-done = f32[2,32,4096]{2,0,1:T(2,128)S(1)} async-done(((f32[2,32,4096]{2,0,1:T(2,128)}), f32[2,32,4096]{2,0,1:T(2,128)S(1)}, u32[]{:S(2)}, u32[]{:S(2)}) %all-to-all-start) | async-done | bytes 1048608 | tf_op jit(solution)/shard_map/all_to_all | solution.py:112
  159.6 0.6 copy.48
  160.4 0.5 convolution_bitcast_fusion.1
  161.0 0.8 squeeze.69
  161.8 0.8 squeeze.70
  (72 shorter events, 3.4 us)
Async XLA Ops:
  2.5 0.8 copy-start.15
  10.3 5.0 %collective-permute-start = (f32[5,16,1,2048]{3,2,1,0:T(1,128)S(1)}, f32[5,16,1,2048]{3,2,1,0:T(1,128)S(1)}, u32[]{:S(2)}, u32[]{:S(2)}) collective-permute-start(f32[5,16,1,2048]{3,2,1,0:T(1,128)S(1)} %broadcast_select_fusion.2), channel_id=1, source_target_pairs={{0,1},{1,0},{2,3},{3,2},{4,5},{5,4},{6,7},{7,6},{8,9},{9,8},{10,11... | collective-permute-start | bytes 1966088 | tf_op jit(solution)/shard_map/ppermute | solution.py:20
  17.5 16.2 %collective-permute-start.1 = (f32[5,8,2,2048]{3,2,1,0:T(2,128)S(1)}, f32[5,8,2,2048]{3,2,1,0:T(2,128)S(1)}, u32[]{:S(2)}, u32[]{:S(2)}) collective-permute-start(f32[5,8,2,2048]{3,2,1,0:T(2,128)S(1)} %broadcast_select_fusion.3), channel_id=1, source_target_pairs={{0,2},{2,0},{1,3},{3,1},{4,6},{6,4},{5,7},{7,5},{8,10},{10,8},{9,1... | collective-permute-start | bytes 1966088 | tf_op jit(solution)/shard_map/ppermute | solution.py:20
  39.2 16.7 %collective-permute-start.2 = (f32[5,4,4,2048]{3,1,2,0:T(4,128)S(1)}, f32[5,4,4,2048]{3,1,2,0:T(4,128)S(1)}, u32[]{:S(2)}, u32[]{:S(2)}) collective-permute-start(f32[5,4,4,2048]{3,1,2,0:T(4,128)S(1)} %bitcast_select_fusion.1), channel_id=1, source_target_pairs={{0,4},{4,0},{1,5},{5,1},{2,6},{6,2},{3,7},{7,3},{8,12},{12,8},{9,1... | collective-permute-start | bytes 1966088 | tf_op jit(solution)/shard_map/ppermute | solution.py:20
  58.5 14.3 %collective-permute-start.3 = (f32[5,2,8,2048]{3,2,1,0:T(8,128)S(1)}, f32[5,2,8,2048]{3,2,1,0:T(8,128)S(1)}, u32[]{:S(2)}, u32[]{:S(2)}) collective-permute-start(f32[5,2,8,2048]{3,2,1,0:T(8,128)S(1)} %fusion.5), channel_id=1, source_target_pairs={{0,8},{8,0},{1,9},{9,1},{2,10},{10,2},{3,11},{11,3},{4,12},{12,4},... | collective-permute-start | bytes 1966088 | tf_op jit(solution)/shard_map/ppermute | solution.py:20
  73.0 1.2 copy-start.14
  73.1 14.9 %collective-permute-start.4 = (f32[5,1,16,2048]{3,2,0,1:T(8,128)S(1)}, f32[5,1,16,2048]{3,2,0,1:T(8,128)S(1)}, u32[]{:S(2)}, u32[]{:S(2)}) collective-permute-start(f32[5,1,16,2048]{3,2,0,1:T(8,128)S(1)} %fusion.6), channel_id=1, source_target_pairs={{0,16},{16,0},{1,17},{17,1},{2,18},{18,2},{3,19},{19,3},{4,20},{20... | collective-permute-start | bytes 1966088 | tf_op jit(solution)/shard_map/ppermute | solution.py:20
  91.2 14.8 %collective-permute-start.5 = (f32[5,1,512]{2,1,0:T(1,128)S(1)}, f32[5,1,512]{2,1,0:T(1,128)S(1)}, u32[]{:S(2)}, u32[]{:S(2)}) collective-permute-start(f32[5,1,512]{2,1,0:T(1,128)S(1)} %get-tuple-element.28), channel_id=1, source_target_pairs={{1,0},{2,1},{3,2},{4,3},{5,4},{6,5},{7,6},{8,7},{9,8},{10,9},{11,1... | collective-permute-start | bytes 30728 | tf_op jit(solution)/shard_map/ppermute | solution.py:31
  96.9 9.1 %collective-permute-start.6 = (f32[5,1,512]{2,1,0:T(1,128)S(1)}, f32[5,1,512]{2,1,0:T(1,128)S(1)}, u32[]{:S(2)}, u32[]{:S(2)}) collective-permute-start(f32[5,1,512]{2,1,0:T(1,128)S(1)} %get-tuple-element.29), channel_id=1, source_target_pairs={{0,1},{1,2},{2,3},{3,4},{4,5},{5,6},{6,7},{7,8},{8,9},{9,10},{10,1... | collective-permute-start | bytes 30728 | tf_op jit(solution)/shard_map/ppermute | solution.py:28
  100.7 2.9 %copy-start.13 = (f32[1,1,2,16,2048]{4,3,0,2,1:T(8,128)S(1)}, f32[1,1,2,16,2048]{4,3,0,2,1:T(8,128)}, u32[]{:S(2)}) copy-start(f32[1,1,2,16,2048]{4,3,0,2,1:T(8,128)} %get-tuple-element.26) | copy-start | bytes 786436
  101.8 4.4 %copy-start.2 = (f32[128,512]{1,0:T(8,128)}, f32[128,512]{1,0:T(8,128)S(1)}, u32[]{:S(2)}) copy-start(f32[128,512]{1,0:T(8,128)S(1)} %slice.242) | copy-start | bytes 786436
  106.0 0.9 copy-start.4
  106.0 1.0 copy-start.6
  107.1 0.9 copy-start
  108.0 0.9 copy-start.3
  108.0 1.9 %copy-start.12 = (f32[1,128,512]{2,1,0:T(8,128)S(1)}, f32[1,128,512]{2,1,0:T(8,128)}, u32[]{:S(2)}) copy-start(f32[1,128,512]{2,1,0:T(8,128)} %slice.261) | copy-start | bytes 786436
  108.1 7.5 %copy-start.16 = (s32[32]{0:T(128)S(1)}, s32[32]{0:T(128)}, u32[]{:S(2)}) copy-start(s32[32]{0:T(128)} %param.9) | copy-start | bytes 388
  109.9 17.4 %copy-start.1 = (f32[128,512]{1,0:T(8,128)S(1)}, f32[128,512]{1,0:T(8,128)}, u32[]{:S(2)}) copy-start(f32[128,512]{1,0:T(8,128)} %slice.251) | copy-start | bytes 786436
  109.9 17.2 %collective-permute-start.7 = (f32[5,1,512]{2,1,0:T(1,128)S(1)}, f32[5,1,512]{2,1,0:T(1,128)S(1)}, u32[]{:S(2)}, u32[]{:S(2)}) collective-permute-start(f32[5,1,512]{2,1,0:T(1,128)S(1)} %get-tuple-element.20), channel_id=1, source_target_pairs={{1,0},{2,1},{3,2},{4,3},{5,4},{6,5},{7,6},{8,7},{9,8},{10,9},{11,1... | collective-permute-start | bytes 30728 | tf_op jit(solution)/shard_map/ppermute | solution.py:31
  112.0 15.2 %collective-permute-start.8 = (f32[5,1,512]{2,1,0:T(1,128)S(1)}, f32[5,1,512]{2,1,0:T(1,128)S(1)}, u32[]{:S(2)}, u32[]{:S(2)}) collective-permute-start(f32[5,1,512]{2,1,0:T(1,128)S(1)} %get-tuple-element.21), channel_id=1, source_target_pairs={{0,1},{1,2},{2,3},{3,4},{4,5},{5,6},{6,7},{7,8},{8,9},{9,10},{10,1... | collective-permute-start | bytes 30728 | tf_op jit(solution)/shard_map/ppermute | solution.py:28
  116.5 18.7 %all-to-all-start.1 = ((f32[1,32,2]{2,0,1:T(1,128)}), f32[1,32,2]{2,0,1:T(1,128)S(1)}, u32[]{:S(2)}, u32[]{:S(2)}) async-start(f32[1,32,2]{2,0,1:T(1,128)} %bitcast.37), calls=%async_computation.1 | async-start | bytes 32768 | tf_op jit(solution)/shard_map/all_to_all | solution.py:115
  127.3 2.6 %copy-start.5 = (f32[128,512]{1,0:T(8,128)S(1)}, f32[128,512]{1,0:T(8,128)}, u32[]{:S(2)}) copy-start(f32[128,512]{1,0:T(8,128)} %slice.248) | copy-start | bytes 786436
  127.3 2.6 %copy-start.7 = (f32[128,512]{1,0:T(8,128)S(1)}, f32[128,512]{1,0:T(8,128)}, u32[]{:S(2)}) copy-start(f32[128,512]{1,0:T(8,128)} %mul.116) | copy-start | bytes 786436
  130.1 1.0 copy-start.9
  131.3 1.0 copy-start.8
  135.2 8.8 %copy-start.10 = (f32[1,128,512]{2,1,0:T(8,128)S(1)}, f32[1,128,512]{2,1,0:T(8,128)}, u32[]{:S(2)}) copy-start(f32[1,128,512]{2,1,0:T(8,128)} %get-tuple-element.36) | copy-start | bytes 786436
  135.2 8.9 %copy-start.11 = (f32[1,128,512]{2,1,0:T(8,128)S(1)}, f32[1,128,512]{2,1,0:T(8,128)}, u32[]{:S(2)}) copy-start(f32[1,128,512]{2,1,0:T(8,128)} %get-tuple-element.37) | copy-start | bytes 786436
  135.2 24.4 %all-to-all-start = ((f32[2,32,4096]{2,0,1:T(2,128)}), f32[2,32,4096]{2,0,1:T(2,128)S(1)}, u32[]{:S(2)}, u32[]{:S(2)}) async-start(f32[2,32,4096]{2,0,1:T(2,128)} %copy.47), calls=%async_computation | async-start | bytes 2097152 | tf_op jit(solution)/shard_map/all_to_all | solution.py:112
where the time goes:
time: 165 us; the launch traced here: 163 us
  waiting for transfers between devices  75.3 us (46%)
  starting transfers between devices  38.4 us (23%)
  local copies, waits for them, and re-layouts  27.9 us (17%)
  other arithmetic  18.3 us (11%)
    ppermute x5, waiting for transfers between devices, from_partner(): return lax.ppermute(block, axis, route)  60.6 us
    all_to_all x1, waiting for transfers between devices, shards(): lax.all_to_all(outgoing.reshape(2, nbis, CAP * flat), 'bis', split_axis=1...  14.7 us
    all_to_all x1, starting transfers between devices, shards(): lax.all_to_all(labels.reshape(1, nbis, CAP), 'bis', split_axis=1, concat_...  10.6 us
    ppermute x2, starting transfers between devices, with_halo(): lax.ppermute(lax.slice_in_dim(block, 0, width, axis=dim), axis, backward)  7.76 us
    all_to_all x1, starting transfers between devices, shards(): lax.all_to_all(outgoing.reshape(2, nbis, CAP * flat), 'bis', split_axis=1...  7.52 us
    ppermute x2, starting transfers between devices, with_halo(): lax.ppermute(lax.slice_in_dim(block, block.shape[dim] - width, None, axis...  6.51 us
    ppermute x5, starting transfers between devices, from_partner(): return lax.ppermute(block, axis, route)  6.07 us
    another operation x8, other arithmetic, shards(): moved = jnp.stack([lower, upper], axis=2).reshape(5, nbis, flat)  4.5 us
  transfers between devices with their start and end apart: 11, of which 6 were waited for; matrix products, arithmetic and copies ran while one was open for 10% of the time, Pallas kernels for 0%

commit v1 on v0

v1 whole, which is shorter than its diff:
```python
import functools

import jax
import jax.numpy as jnp
from jax import lax
from jax.experimental import pallas as pl
from jax.experimental.pallas import tpu as pltpu
from jax.sharding import PartitionSpec as P

DT = 0.15
NB = 32
NG = 8
W = 512
LANE = 128
SPLIT = W // LANE
BLK = 4 * SPLIT
BASE = 16
EXT = BASE + NB * BLK + 16
MESH = pl.DeviceIdType.MESH
STRIDE = 11


def neighbour(me, k):
    j = lax.rem(k * STRIDE, NB)
    x, y, c = me // 8, lax.rem(me // 2, 4), lax.rem(me, 2)
    dx, dy, dc = j // 8, lax.rem(j // 2, 4), lax.rem(j, 2)
    return lax.rem(x + dx, 4) * 8 + lax.rem(y + dy, 4) * 2 + lax.rem(c + dc, 2)


def rows_of(block):
    return pl.multiple_of(BASE + block * BLK, 8)


def step_block(at, size, rho_ref, ene_ref, velu_ref, velv_ref, gam, press_ref):
    lane = lax.broadcasted_iota(jnp.int32, (size, LANE), 1)
    piece = lax.rem(lax.broadcasted_iota(jnp.int32, (size, LANE), 0), SPLIT)

    def ld(ref, off):
        return ref[pl.ds(at + off, size), :]

    def columns(ref):
        here = ld(ref, 0)
        before = jnp.where(piece == 0, 0.0, ld(ref, -1))
        after = jnp.where(piece == SPLIT - 1, 0.0, ld(ref, 1))
        left = pltpu.roll(jnp.where(lane == LANE - 1, before, here), 1, 1)
        right = pltpu.roll(jnp.where(lane == 0, after, here), LANE - 1, 1)
        return right - left

    dens = ld(rho_ref, 0)
    ene = ld(ene_ref, 0)
    grad_x = 0.5 * (ld(press_ref, SPLIT) - ld(press_ref, -SPLIT))
    grad_y = 0.5 * columns(press_ref)
    spread = 0.5 * (ld(velu_ref, SPLIT) - ld(velu_ref, -SPLIT) + columns(velv_ref))
    growth = 1.0 + DT * spread
    inverse = 1.0 / dens
    return (
        dens / growth,
        ene * (1.0 - DT * (gam - 1.0) * spread),
        ld(velu_ref, 0) - DT * grad_x * inverse,
        ld(velv_ref, 0) - DT * grad_y * inverse,
        growth,
    )


def main_kernel(
    order_ref, plan_ref, state_ref, meta_ref, sweep_ref,
    arr_ref, got_ref, vel_ref,
    xv, lin, snd, ext, press, one, snd2, part, swl, vel,
    in_sem, s1, r1, sm, rm, sh, rh, s2, r2, out_sem,
):
    grp = lax.axis_index("grp")
    me = lax.axis_index("bis")
    whole = grp * NB + me
    has_low = whole > 0
    has_high = whole < NG * NB - 1
    low = (grp - (me == 0).astype(jnp.int32), lax.rem(me + NB - 1, NB))
    high = (grp + (me == NB - 1).astype(jnp.int32), lax.rem(me + 1, NB))
    far_low = jnp.logical_and(me == 0, has_low)
    far_high = jnp.logical_and(me == NB - 1, has_high)

    barrier = pltpu.get_barrier_semaphore()

    loads = [
        pltpu.make_async_copy(state_ref.at[f], xv.at[f], in_sem.at[f]) for f in range(5)
    ]
    for load in loads:
        load.start()

    def greet(k, carry):
        pl.semaphore_signal(
            barrier, inc=1, device_id=(grp, neighbour(me, k)), device_id_type=MESH
        )
        return carry

    lax.fori_loop(1, NB, greet, 0)

    @pl.when(far_low)
    def _():
        pl.semaphore_signal(barrier, inc=1, device_id=low, device_id_type=MESH)

    @pl.when(far_high)
    def _():
        pl.semaphore_signal(barrier, inc=1, device_id=high, device_id_type=MESH)

    flat = lin.reshape(5, NB * BLK, LANE)
    for f in range(5):
        loads[f].wait()
        for i in range(16):
            for c in range(SPLIT):
                flat[f, pl.ds(i * 8 * SPLIT + c, 8, stride=SPLIT), :] = xv[
                    f, i * 8 : i * 8 + 8, c * LANE : c * LANE + LANE
                ]

    def picked(d):
        return lin[:, order_ref[0, d]]

    def pack(k):
        d = neighbour(me, k)
        snd[d] = picked(d)

    pl.semaphore_wait(
        barrier, NB - 1 + far_low.astype(jnp.int32) + far_high.astype(jnp.int32)
    )

    def move(d, source):
        return pltpu.make_async_remote_copy(
            src_ref=snd.at[d],
            dst_ref=ext.at[:, pl.ds(rows_of(source), BLK), :],
            send_sem=s1.at[d],
            recv_sem=r1.at[source],
            device_id=(grp, d),
            device_id_type=MESH,
        )

    def tell(d, source):
        return pltpu.make_async_remote_copy(
            src_ref=meta_ref,
            dst_ref=got_ref.at[source],
            send_sem=sm.at[d],
            recv_sem=rm.at[source],
            device_id=(grp, d),
            device_id_type=MESH,
        )

    pack(1)

    def send(k, carry):
        @pl.when(k < NB - 1)
        def _():
            pack(k + 1)

        move(neighbour(me, k), me).start()
        return carry

    lax.fori_loop(1, NB, send, 0)

    def send_meta(k, carry):
        tell(neighbour(me, k), me).start()
        return carry

    lax.fori_loop(1, NB, send_meta, 0)
    own_meta = pltpu.make_async_copy(meta_ref, got_ref.at[me], out_sem.at[2])
    own_meta.start()

    ext[:, pl.ds(rows_of(me), BLK), :] = picked(me)
    zero = jnp.zeros((8, LANE), jnp.float32)
    for f in range(5):
        ext[f, 0:8, :] = zero
        ext[f, EXT - 8 : EXT, :] = zero

    @pl.when(jnp.logical_not(has_low))
    def _():
        for f in range(5):
            ext[f, 8:16, :] = zero

    @pl.when(jnp.logical_not(has_high))
    def _():
        for f in range(5):
            ext[f, EXT - 16 : EXT - 8, :] = zero

    press[0, 0:8, :] = zero
    press[0, EXT - 8 : EXT, :] = zero
    for i in range(16):
        for c in range(SPLIT):
            swl[pl.ds(i * 8 * SPLIT + c, 8, stride=SPLIT), :] = sweep_ref[
                i * 8 : i * 8 + 8, c * LANE : c * LANE + LANE
            ]

    def pressure(at, size):
        rows = pl.ds(at, size)
        press[0, rows, :] = (ext[4, rows, :] - 1.0) * ext[0, rows, :] * ext[1, rows, :]

    pressure(rows_of(me), BLK)

    def arrive(k, carry):
        source = neighbour(me, k)
        move(source, source).wait_recv()
        pressure(rows_of(source), BLK)
        return carry

    lax.fori_loop(1, NB, arrive, 0)

    up = pltpu.make_async_remote_copy(
        src_ref=ext.at[:, pl.ds(EXT - 24, 8), :],
        dst_ref=ext.at[:, pl.ds(8, 8), :],
        send_sem=sh.at[0],
        recv_sem=rh.at[0],
        device_id=high,
        device_id_type=MESH,
    )
    down = pltpu.make_async_remote_copy(
        src_ref=ext.at[:, pl.ds(BASE, 8), :],
        dst_ref=ext.at[:, pl.ds(EXT - 16, 8), :],
        send_sem=sh.at[1],
        recv_sem=rh.at[1],
        device_id=low,
        device_id_type=MESH,
    )

    @pl.when(has_high)
    def _():
        up.start()

    @pl.when(has_low)
    def _():
        down.start()

    def first(at, size, keep=None):
        gam = ext[4, pl.ds(at, size), :]
        rho, ene, velu, velv, growth = step_block(
            at, size, ext.at[0], ext.at[1], ext.at[2], ext.at[3], gam, press.at[0]
        )
        pre = (gam - 1.0) * rho * ene
        if keep is not None:
            velu = jnp.where(keep, velu, 0.0)
            pre = jnp.where(keep, pre, 0.0)
        rows = pl.ds(at, size)
        one[0, rows, :] = rho
        one[1, rows, :] = ene
        one[2, rows, :] = velu
        one[3, rows, :] = velv
        one[4, rows, :] = growth
        press[1, rows, :] = pre

    def second(block):
        at = rows_of(block)
        gam = ext[4, pl.ds(at, BLK), :]
        rho, ene, velu, velv, growth = step_block(
            at, BLK, one.at[0], one.at[1], one.at[2], one.at[3], gam, press.at[1]
        )
        volume = one[4, pl.ds(at, BLK), :] * growth
        here = pl.multiple_of(block * BLK, BLK)
        vel[0, pl.ds(here, BLK), :] = velu
        vel[1, pl.ds(here, BLK), :] = velv
        mass = rho * volume
        heat = mass * ene
        frac = swl[pl.ds(here, BLK), :] * volume / (1.0 + volume)
        part[block, 0] = (1.0 - frac) * mass + pltpu.roll(frac * mass, SPLIT, 0)
        part[block, 1] = (1.0 - frac) * heat + pltpu.roll(frac * heat, SPLIT, 0)

    def first_loop(b, carry):
        first(rows_of(b), BLK)
        return carry

    def second_loop(b, carry):
        second(b)
        return carry

    lax.fori_loop(1, NB - 1, first_loop, 0)
    lax.fori_loop(2, NB - 2, second_loop, 0)

    @pl.when(has_low)
    def _():
        up.wait_recv()

    @pl.when(has_high)
    def _():
        down.wait_recv()

    pressure(8, 8)
    pressure(EXT - 16, 8)
    first(8, 8, has_low)
    first(EXT - 16, 8, has_high)

    def edge_first(j, carry):
        first(rows_of(j * (NB - 1)), BLK)
        return carry

    lax.fori_loop(0, 2, edge_first, 0)

    def edge_second(j, carry):
        second(j + (j // 2) * (NB - 4))
        return carry

    lax.fori_loop(0, 4, edge_second, 0)

    vel_out = pltpu.make_async_copy(vel, vel_ref, out_sem.at[0])

    def share(d, source):
        return pltpu.make_async_remote_copy(
            src_ref=snd2.at[d],
            dst_ref=arr_ref.at[source],
            send_sem=s2.at[d],
            recv_sem=r2.at[source],
            device_id=(grp, d),
            device_id_type=MESH,
        )

    def pack2(d):
        snd2[d, 0] = part[plan_ref[0, 64 + d]]
        snd2[d, 1] = part[plan_ref[0, 96 + d]]

    pack2(neighbour(me, 1))

    def send2(k, carry):
        @pl.when(k < NB - 1)
        def _():
            pack2(neighbour(me, k + 1))

        share(neighbour(me, k), me).start()
        return carry

    lax.fori_loop(1, NB, send2, 0)
    pack2(me)
    vel_out.start()
    own = pltpu.make_async_copy(snd2.at[me], arr_ref.at[me], out_sem.at[1])
    own.start()

    def finish(k, carry):
        d = neighbour(me, k)
        move(d, me).wait_send()
        tell(d, me).wait_send()
        tell(d, d).wait_recv()
        return carry

    lax.fori_loop(1, NB, finish, 0)

    @pl.when(has_high)
    def _():
        up.wait_send()

    @pl.when(has_low)
    def _():
        down.wait_send()

    def finish2(k, carry):
        d = neighbour(me, k)
        share(d, d).wait_recv()
        share(d, me).wait_send()
        return carry

    lax.fori_loop(1, NB, finish2, 0)
    own_meta.wait()
    vel_out.wait()
    own.wait()


def last_kernel(got_ref, arr_ref, vel_ref, mass_ref, heat_ref, velo_ref, acc):
    me = lax.axis_index("bis")
    for q in range(2):
        acc[q] = jnp.zeros(acc.shape[1:], jnp.float32)

    def add(source, carry):
        for k in range(2):
            at = pl.multiple_of(got_ref[source, 0, k * NB + me] * BLK, BLK)
            for q in range(2):
                acc[q, pl.ds(at, BLK), :] += arr_ref[source, k, q]
        return carry

    lax.fori_loop(0, NB, add, 0)
    for i in range(16):
        for c in range(SPLIT):
            rows = pl.ds(i * 8 * SPLIT + c, 8, stride=SPLIT)
            put = (slice(i * 8, i * 8 + 8), slice(c * LANE, c * LANE + LANE))
            mass_ref[put] = acc[0, rows, :]
            heat_ref[put] = acc[1, rows, :]
            velo_ref[(0,) + put] = vel_ref[0, rows, :]
            velo_ref[(1,) + put] = vel_ref[1, rows, :]


def shards(state, order, sweep, owner, slot_target):
    f32 = jnp.float32
    index = jnp.arange(NB, dtype=jnp.int32)
    code = index * NB + slot_target
    hit = owner == index[None, :]
    low = jnp.min(jnp.where(hit, code[:, None], NB * NB), axis=0)
    high = jnp.max(jnp.where(hit, code[:, None], -1), axis=0)
    plan = jnp.concatenate(
        [
            jnp.where(low < NB * NB, low % NB, NB),
            jnp.where(high > low, high % NB, NB),
            jnp.minimum(low // NB, NB - 1),
            jnp.maximum(high, 0) // NB,
        ]
    ).reshape(1, 4 * NB)
    any_ = pl.BlockSpec(memory_space=pl.ANY)
    vmem = pl.BlockSpec(memory_space=pltpu.VMEM)
    smem = pl.BlockSpec(memory_space=pltpu.SMEM)
    dma = pltpu.SemaphoreType.DMA
    arrived, got, vel = pl.pallas_call(
        main_kernel,
        name="step",
        out_shape=(
            jax.ShapeDtypeStruct((NB, 2, 2, BLK, LANE), f32),
            jax.ShapeDtypeStruct((NB, 1, LANE), jnp.int32),
            jax.ShapeDtypeStruct((2, NB * BLK, LANE), f32),
        ),
        in_specs=[smem, smem, any_, any_, vmem],
        out_specs=(any_, any_, any_),
        scratch_shapes=[
            pltpu.VMEM((5, 128, W), f32),
            pltpu.VMEM((5, NB, BLK, LANE), f32),
            pltpu.VMEM((NB, 5, BLK, LANE), f32),
            pltpu.VMEM((5, EXT, LANE), f32),
            pltpu.VMEM((2, EXT, LANE), f32),
            pltpu.VMEM((5, EXT, LANE), f32),
            pltpu.VMEM((NB, 2, 2, BLK, LANE), f32),
            pltpu.VMEM((NB, 2, BLK, LANE), f32),
            pltpu.VMEM((NB * BLK, LANE), f32),
            pltpu.VMEM((2, NB * BLK, LANE), f32),
            dma((5,)),
            dma((NB,)), dma((NB,)),
            dma((NB,)), dma((NB,)),
            dma((2,)), dma((2,)),
            dma((NB,)), dma((NB,)),
            dma((3,)),
        ],
        compiler_params=pltpu.CompilerParams(collective_id=0, has_side_effects=True),
    )(order, plan, state, plan, sweep)
    shape = jax.ShapeDtypeStruct((128, W), f32)
    return pl.pallas_call(
        last_kernel,
        name="gather",
        out_shape=(shape, shape, jax.ShapeDtypeStruct((2, 128, W), f32)),
        in_specs=[smem, vmem, vmem],
        out_specs=(vmem, vmem, vmem),
        scratch_shapes=[pltpu.VMEM((2, (NB + 1) * BLK, LANE), f32)],
    )(got, arrived, vel)


def solution(mesh):
    rows = P(("grp", "bis"), None)
    return jax.shard_map(
        shards,
        mesh=mesh,
        in_specs=(P(None, ("grp", "bis"), None), rows, rows, rows, P(("grp", "bis"))),
        out_specs=(rows, rows, P(None, ("grp", "bis"), None)),
        check_vma=False,
    )
```

time: 165 us -> 55.5 us (0.34); the launches traced: 163 us -> 55.3 us
  waiting for transfers between devices: 75.3 us -> 0 us
  Pallas kernels: 0 us -> 52.6 us
  starting transfers between devices: 38.4 us -> 0 us
  local copies, waits for them, and re-layouts: 27.9 us -> 0 us
  other arithmetic: 18.3 us -> 2.01 us
    ppermute x9 -> x0, waiting for transfers between devices: 60.6 us -> none  [the longest x5 60.6 us: from_partner(): return lax.ppermute(block, axis, route)]
    pallas_call x0 -> x2, Pallas kernels: none -> 52.6 us  [the longest x1 49.8 us: shards(): pl.pallas_call(main_kernel, name='step', out_shape=(jax.ShapeDtypeStruct(...]
    ppermute x9 -> x0, starting transfers between devices: 20.3 us -> none  [the longest x2 7.76 us: with_halo(): lax.ppermute(lax.slice_in_dim(block, 0, width, axis=dim), axis, backward)]
    all_to_all x2 -> x0, starting transfers between devices: 18.1 us -> none  [the longest x1 10.6 us: shards(): lax.all_to_all(labels.reshape(1, nbis, CAP), 'bis', split_axis=1, concat_...]
    all_to_all x2 -> x0, waiting for transfers between devices: 14.7 us -> none  [the longest x1 14.7 us: shards(): lax.all_to_all(outgoing.reshape(2, nbis, CAP * flat), 'bis', split_axis=1...]
    another operation x12 -> x0, other arithmetic: 8.09 us -> none  [the longest x8 4.5 us: shards(): moved = jnp.stack([lower, upper], axis=2).reshape(5, nbis, flat)]
    select_n x8 -> x1, other arithmetic: 6.43 us -> 0.01 us  [shards(): jnp.where(low < NB * NB, low % NB, NB)]
    slice x11 -> x0, local copies, waits for them, and re-layouts: 6.14 us -> none  [the longest x1 1.82 us: advance(): ene[1:-1] * (1.0 - STEP_DT * (center_g - 1.0) * spread)]
  transfers between devices with their start and end apart: 11 -> 0, of which waited for: 6 -> 0; matrix products, arithmetic and copies ran while one was open for 10% -> 0% of each run, Pallas kernels for 0% -> 0%
where the time goes in v1:
time: 55.5 us; the launch traced here: 55.3 us
  Pallas kernels  52.6 us (95%)
  other arithmetic  2.01 us (4%)
  between operations  0.65 us (1%)
    pallas_call x1, Pallas kernels, shards(): pl.pallas_call(main_kernel, name='step', out_shape=(jax.ShapeDtypeStruct(...  49.8 us
    pallas_call x1, Pallas kernels, shards(): pl.pallas_call(last_kernel, name='gather', out_shape=(shape, shape, jax.S...  2.86 us

profile of v1, /device:TPU:1, one launch (start us, length us, event | category | flops | bytes accessed | tf_op | source)
XLA Modules:
  0.0 55.3 jit_solution(6385417627595037005)
XLA Ops:
  0.6 0.7 %multiply_add_fusion = s32[32]{0:T(128)S(1)} fusion(s32[32]{0:T(128)} %param.9), kind=kLoop, calls=%fused_computation.16 | loop fusion | flops 64 | bytes 256 | tf_op jit(solution)/shard_map/add | solution.py:384
  1.3 0.7 %select_reduce_fusion.1 = (s32[32]{0:T(128)S(1)}, s32[32]{0:T(128)S(1)}) fusion(s32[32]{0:T(128)S(1)} %multiply_add_fusion, s32[32]{0:T(128)} %bitcast.3), kind=kLoop, calls=%fused_computation.1 | loop fusion | flops 5056 | bytes 512 | tf_op jit(solution)/shard_map/reduce_min | solution.py:386
  2.1 0.6 %add_bitcast_fusion.plan_ref.meta_ref = s32[1,128]{1,0:T(1,128)} fusion(s32[32]{0:T(128)S(1)} %get-tuple-element.14, s32[32]{0:T(128)S(1)} %get-tuple-element.12, s32[32]{0:T(128)S(1)} %get-tuple-element.13, s32[32]{0:T(128)S(1)} %get-tuple-element.11), kind=kLoop, calls=%fused_computation.15 | loop fusion | flops 384 | bytes 1024 | tf_op jit(solution)/shard_map/reshape | solution.py:395
  2.6 49.8 %step.1 = (f32[32,2,2,16,128]{4,3,2,1,0:T(8,128)}, s32[32,1,128]{2,1,0:T(1,128)}, f32[2,512,128]{2,1,0:T(8,128)}) custom-call(s32[1,32]{1,0:T(1,128)} %order_ref.1, s32[1,128]{1,0:T(1,128)} %add_bitcast_fusion.plan_ref.meta_ref, f32[5,128,512]{2,1,0:T(8,128)} %state_ref.1, s32[1,128]{1,0:T(1,128)} %add_bitcast_fusion.plan_ref.meta_ref, f32[128,512]{1,0:T(8,128)} %sweep_ref.1), custom_call_target="tpu_custom_call" | custom-call | tf_op jit(solution)/shard_map/step/pallas_call | solution.py:400
  52.4 2.9 %gather.1 = (f32[128,512]{1,0:T(8,128)}, f32[128,512]{1,0:T(8,128)}, f32[2,128,512]{2,1,0:T(8,128)}) custom-call(s32[32,1,128]{2,1,0:T(1,128)} %get-tuple-element.6.got_ref, f32[32,2,2,16,128]{4,3,2,1,0:T(8,128)} %get-tuple-element.7.arr_ref, f32[2,512,128]{2,1,0:T(8,128)} %get-tuple-element.8.vel_ref), custom_call_target="tpu_custom_call" | custom-call | tf_op jit(solution)/shard_map/gather/pallas_call | solution.py:431
  (1 shorter events, 0.0 us)

commit v2 on v0

v2 whole, which is shorter than its diff:
```python
import jax
import jax.numpy as jnp
from jax import lax
from jax.experimental import pallas as pl
from jax.experimental.pallas import tpu as pltpu
from jax.sharding import PartitionSpec as P

DT = 0.15
NB = 32
NG = 8
W = 512
ROWS = 128
BR = 4
LANE = 128
PIECES = W // LANE
EARLY = 3
LATE = PIECES - EARLY
TOP = 16
EXT = TOP + ROWS + 16
MESH = pl.DeviceIdType.MESH
STRIDE = 13
HOLD = 16
F32 = jnp.float32


def neighbour(me, k):
    j = lax.rem(k * STRIDE, NB)
    x, y, c = me // 8, lax.rem(me // 2, 4), lax.rem(me, 2)
    dx, dy, dc = j // 8, lax.rem(j // 2, 4), lax.rem(j, 2)
    return lax.rem(x + dx, 4) * 8 + lax.rem(y + dy, 4) * 2 + lax.rem(c + dc, 2)


def lane_mask(size, lane):
    return lax.broadcasted_iota(jnp.int32, (size, LANE), 1) == lane


def advance(piece, at, size, fields, press, closed):
    def ld(ref, off=0, where=piece):
        return ref[where, pl.ds(at + off, size), :]

    def columns(ref):
        here = ld(ref)
        before = ld(ref, 0, piece - 1) if piece > 0 else 0.0
        after = ld(ref, 0, piece + 1) if piece + 1 < PIECES and not closed else 0.0
        left = pltpu.roll(jnp.where(lane_mask(size, LANE - 1), before, here), 1, 1)
        right = pltpu.roll(jnp.where(lane_mask(size, 0), after, here), LANE - 1, 1)
        return right - left

    rho, ene, velu, velv, gam = fields
    dens = ld(rho)
    grad_x = 0.5 * (ld(press, 1) - ld(press, -1))
    grad_y = 0.5 * columns(press)
    spread = 0.5 * (ld(velu, 1) - ld(velu, -1) + columns(velv))
    growth = 1.0 + DT * spread
    inverse = 1.0 / dens
    gamma = ld(gam)
    return (
        dens / growth,
        ld(ene) * (1.0 - DT * (gamma - 1.0) * spread),
        ld(velu) - DT * grad_x * inverse,
        ld(velv) - DT * grad_y * inverse,
        growth,
        gamma,
    )


def main_kernel(
    order_ref, owner_ref, slot_ref, state_ref, sweep_ref,
    arr_a, arr_b, got_ref, vel_ref,
    xv, lin_a, lin_b, snd_a, snd_b, msg_a, msg_b, hal_a, hal_b,
    ext, one, press0, press1, part_a, part_b, out_a, out_b, vel, plan_v, plan_s,
    in_sem, s1a, r1a, s1b, r1b, sm, rm, sh, rh, s2a, r2a, s2b, r2b, loc,
):
    grp = lax.axis_index("grp")
    me = lax.axis_index("bis")
    whole = grp * NB + me
    has_low = whole > 0
    has_high = whole < NG * NB - 1
    first_one = me == 0
    last_one = me == NB - 1
    low = (grp - first_one.astype(jnp.int32), lax.rem(me + NB - 1, NB))
    high = (grp + last_one.astype(jnp.int32), lax.rem(me + 1, NB))
    far_low = jnp.logical_and(first_one, has_low)
    far_high = jnp.logical_and(last_one, has_high)

    loads = [pltpu.make_async_copy(state_ref.at[f], xv.at[f], in_sem.at[f]) for f in range(5)]
    for load in loads:
        load.start()

    barrier = pltpu.get_barrier_semaphore()

    def loop(lo, hi, body):
        def step(k, carry):
            body(k)
            return carry

        lax.fori_loop(lo, hi, step, 0)

    def greet(k):
        pl.semaphore_signal(
            barrier, inc=1, device_id=(grp, neighbour(me, k)), device_id_type=MESH
        )

    loop(1, NB, greet)

    @pl.when(far_low)
    def _():
        pl.semaphore_signal(barrier, inc=1, device_id=low, device_id_type=MESH)

    @pl.when(far_high)
    def _():
        pl.semaphore_signal(barrier, inc=1, device_id=high, device_id_type=MESH)

    row = lax.broadcasted_iota(jnp.int32, (NB, LANE), 0)
    lane = lax.broadcasted_iota(jnp.int32, (NB, LANE), 1)
    same = lax.broadcasted_iota(jnp.int32, (NB, NB), 0) == lax.broadcasted_iota(
        jnp.int32, (NB, NB), 1
    )

    def column(ref):
        spread = jnp.where(same, jnp.broadcast_to(ref[...], (NB, NB)), 0)
        return jnp.sum(spread, axis=1, keepdims=True)

    code = row * NB + column(slot_ref)
    hit = jnp.broadcast_to(column(owner_ref), (NB, LANE)) == lax.rem(lane, NB)
    least = jnp.min(jnp.where(hit, code, NB * NB), axis=0, keepdims=True)
    most = jnp.max(jnp.where(hit, code, -1), axis=0, keepdims=True)
    at_lane = lax.broadcasted_iota(jnp.int32, (1, LANE), 1)
    plan_v[...] = jnp.where(
        at_lane < NB,
        jnp.where(least < NB * NB, least & (NB - 1), NB),
        jnp.where(
            at_lane < 2 * NB,
            jnp.where(most > least, most & (NB - 1), NB),
            jnp.where(
                at_lane < 3 * NB,
                jnp.minimum(least >> 5, NB - 1),
                jnp.maximum(most, 0) >> 5,
            ),
        ),
    )

    for f in range(5):
        loads[f].wait()
        for c in range(PIECES):
            for b in range(NB):
                half = xv[f, b * BR : b * BR + BR, c * LANE : c * LANE + LANE]
                if c < EARLY:
                    lin_a[b, f, c] = half
                else:
                    lin_b[b, f, c - EARLY] = half

    plan_copy = pltpu.make_async_copy(plan_v, plan_s, loc.at[0])
    plan_copy.start()
    pl.semaphore_wait(
        barrier, NB - 1 + far_low.astype(jnp.int32) + far_high.astype(jnp.int32)
    )

    def remote(src, dst, send, recv, d):
        return pltpu.make_async_remote_copy(
            src_ref=src, dst_ref=dst, send_sem=send, recv_sem=recv,
            device_id=(grp, d), device_id_type=MESH,
        )

    def move_a(d, source):
        return remote(snd_a.at[d], msg_a.at[source], s1a.at[d], r1a.at[source], d)

    def move_b(d, source):
        return remote(snd_b.at[d], msg_b.at[source], s1b.at[d], r1b.at[source], d)

    def tell(d, source):
        return remote(plan_v, got_ref.at[source], sm.at[d], rm.at[source], d)

    def share_a(d, source):
        return remote(out_a.at[d], arr_a.at[source], s2a.at[d], r2a.at[source], d)

    def share_b(d, source):
        return remote(out_b.at[d], arr_b.at[source], s2b.at[d], r2b.at[source], d)

    def fill_a(k):
        d = neighbour(me, k)
        snd_a[d] = lin_a[order_ref[0, d]]

    def fill_b(k):
        d = neighbour(me, k)
        snd_b[d] = lin_b[order_ref[0, d]]

    fill_a(1)

    def go_a(k):
        @pl.when(k < NB - 1)
        def _():
            fill_a(k + 1)

        move_a(neighbour(me, k), me).start()

    loop(1, NB, go_a)
    loop(1, NB, fill_b)
    loop(1, NB - HOLD, lambda k: move_b(neighbour(me, k), me).start())
    loop(1, NB, lambda k: tell(neighbour(me, k), me).start())
    own_plan = pltpu.make_async_copy(plan_v, got_ref.at[me], loc.at[1])
    own_plan.start()
    msg_a[me] = lin_a[order_ref[0, me]]
    msg_b[me] = lin_b[order_ref[0, me]]

    zero = jnp.zeros((TOP, LANE), F32)
    for c in range(PIECES):
        for f in range(5):
            ext[f, c, 0:TOP, :] = zero
            ext[f, c, EXT - 16 : EXT, :] = zero
        press0[c, 0:TOP, :] = zero
        press0[c, EXT - 16 : EXT, :] = zero

    def spread_out(values, c, at):
        for f in range(5):
            ext[f, c, pl.ds(at, BR), :] = values[f]
        press0[c, pl.ds(at, BR), :] = (values[4] - 1.0) * values[0] * values[1]

    def unpack(msg, base, count, source):
        for c in range(count):
            spread_out([msg[source, f, c] for f in range(5)], base + c, TOP + source * BR)

    def halo(hal, msg, at):
        up = pltpu.make_async_remote_copy(
            src_ref=msg.at[NB - 1], dst_ref=hal.at[0], send_sem=sh.at[at], recv_sem=rh.at[at],
            device_id=high, device_id_type=MESH,
        )
        down = pltpu.make_async_remote_copy(
            src_ref=msg.at[0], dst_ref=hal.at[1], send_sem=sh.at[at + 1], recv_sem=rh.at[at + 1],
            device_id=low, device_id_type=MESH,
        )
        return up, down

    def pass_on(pair, move):
        up, down = pair

        @pl.when(jnp.logical_not(last_one))
        def _():
            move(NB - 1, NB - 1).wait_recv()

        @pl.when(has_high)
        def _():
            up.start()

        @pl.when(jnp.logical_not(first_one))
        def _():
            move(0, 0).wait_recv()

        @pl.when(has_low)
        def _():
            down.start()

    def collect(move, msg, base, count):
        def one_source(k):
            source = neighbour(me, k)

            @pl.when(jnp.logical_and(source > 0, source < NB - 1))
            def _():
                move(source, source).wait_recv()

            unpack(msg, base, count, source)

        loop(1, NB, one_source)
        unpack(msg, base, count, me)

    def halo_in(pair, hal, base, count):
        up, down = pair

        @pl.when(has_low)
        def _():
            up.wait_recv()
            for c in range(count):
                spread_out([hal[0, f, c] for f in range(5)], base + c, TOP - BR)

        @pl.when(has_high)
        def _():
            down.wait_recv()
            for c in range(count):
                spread_out([hal[1, f, c] for f in range(5)], base + c, TOP + ROWS)

    start = [ext.at[f] for f in range(5)]
    after = [one.at[f] for f in range(4)] + [ext.at[4]]

    def first(pieces, at, size, closed=None, keep=None):
        rows = pl.ds(at, size)
        done = [advance(c, at, size, start, press0, c == closed) for c in pieces]
        for c, (rho, ene, velu, velv, growth, gamma) in zip(pieces, done):
            pre = (gamma - 1.0) * rho * ene
            if keep is not None:
                velu = jnp.where(keep, velu, 0.0)
                pre = jnp.where(keep, pre, 0.0)
            one[0, c, rows, :] = rho
            one[1, c, rows, :] = ene
            one[2, c, rows, :] = velu
            one[3, c, rows, :] = velv
            one[4, c, rows, :] = growth
            press1[c, rows, :] = pre

    def second(pieces, block, size, part):
        mesh_row = pl.multiple_of(block * BR, 8)
        at = pl.multiple_of(TOP + block * BR, 8)
        done = [advance(c, at, size, after, press1, False) for c in pieces]
        head = lax.rem(lax.broadcasted_iota(jnp.int32, (size, LANE), 0), BR) == 0

        def mixed(value, frac):
            away = frac * value
            near = pltpu.roll(away, 1, 0)
            wrap = pltpu.roll(away, size - (BR - 1), 0)
            return (1.0 - frac) * value + jnp.where(head, wrap, near)

        for c, (rho, ene, velu, velv, growth, _) in zip(pieces, done):
            columns = slice(c * LANE, c * LANE + LANE)
            volume = one[4, c, pl.ds(at, size), :] * growth
            vel[0, pl.ds(mesh_row, size), columns] = velu
            vel[1, pl.ds(mesh_row, size), columns] = velv
            mass = rho * volume
            heat = mass * ene
            frac = sweep_ref[pl.ds(mesh_row, size), columns] * volume / (1.0 + volume)
            for q, value in enumerate((mixed(mass, frac), mixed(heat, frac))):
                put = q * 8 + (c % 2) * BR
                for i in range(size // BR):
                    part[block + i, put : put + BR, :] = value[i * BR : i * BR + BR]

    def inner_rows(pieces, closed, results, part):
        loop(0, 7, lambda i: first(pieces, pl.multiple_of(TOP + 8 + i * 16, 8), 16, closed))
        loop(0, 6, lambda i: second(results, 4 + i * 4, 16, part))

    def edge_rows(pieces, closed, results, part):
        first(pieces, TOP - 8, 8, closed, has_low)
        first(pieces, TOP + ROWS, 8, closed, has_high)
        loop(0, 2, lambda j: first(pieces, pl.multiple_of(TOP + j * (ROWS - 8), 8), 8, closed))
        loop(0, 2, lambda j: second(results, j * (NB - 4), 16, part))

    pair_a = halo(hal_a, msg_a, 0)
    pair_b = halo(hal_b, msg_b, 2)

    pass_on(pair_a, move_a)
    loop(NB - HOLD, NB, lambda k: move_b(neighbour(me, k), me).start())
    collect(move_a, msg_a, 0, EARLY)
    early, late = (0, 1), (2, 3)
    inner_rows((0, 1, 2), 2, early, part_a)
    halo_in(pair_a, hal_a, 0, EARLY)
    edge_rows((0, 1, 2), 2, early, part_a)

    plan_copy.wait()

    def fill2(out, part, d):
        out[d, 0] = part[plan_s[0, 2 * NB + d]]
        out[d, 1] = part[plan_s[0, 3 * NB + d]]

    loop(0, NB, lambda d: fill2(out_a, part_a, d))
    loop(1, NB - HOLD, lambda k: share_a(neighbour(me, k), me).start())
    own_a = pltpu.make_async_copy(out_a.at[me], arr_a.at[me], loc.at[2])
    own_a.start()

    pass_on(pair_b, move_b)
    loop(NB - HOLD, NB, lambda k: share_a(neighbour(me, k), me).start())
    collect(move_b, msg_b, EARLY, LATE)
    inner_rows((2, 3), None, late, part_b)
    halo_in(pair_b, hal_b, EARLY, LATE)
    edge_rows((2, 3), None, late, part_b)
    loop(0, NB, lambda d: fill2(out_b, part_b, d))
    loop(1, NB, lambda k: share_b(neighbour(me, k), me).start())
    own_b = pltpu.make_async_copy(out_b.at[me], arr_b.at[me], loc.at[3])
    own_b.start()
    vel_out = pltpu.make_async_copy(vel, vel_ref, loc.at[4])
    vel_out.start()

    def finish(k):
        d = neighbour(me, k)
        move_a(d, me).wait_send()
        move_b(d, me).wait_send()
        tell(d, me).wait_send()
        tell(d, d).wait_recv()
        share_a(d, me).wait_send()
        share_a(d, d).wait_recv()

    loop(1, NB, finish)

    @pl.when(has_high)
    def _():
        pair_a[0].wait_send()
        pair_b[0].wait_send()

    @pl.when(has_low)
    def _():
        pair_a[1].wait_send()
        pair_b[1].wait_send()

    own_plan.wait()
    own_a.wait()
    own_b.wait()
    vel_out.wait()

    def finish_b(k):
        d = neighbour(me, k)
        share_b(d, me).wait_send()
        share_b(d, d).wait_recv()

    loop(1, NB, finish_b)


def last_kernel(
    got_ref, arr_a, arr_b, vel_ref, mass_ref, heat_ref, velo_ref,
    got, arr, vel, acc, out, sem,
):
    me = lax.axis_index("bis")
    ins = [
        pltpu.make_async_copy(got_ref, got, sem.at[0]),
        pltpu.make_async_copy(arr_a, arr.at[0], sem.at[1]),
        pltpu.make_async_copy(arr_b, arr.at[1], sem.at[2]),
        pltpu.make_async_copy(vel_ref, vel, sem.at[3]),
    ]
    for copy in ins:
        copy.start()
    acc[...] = jnp.zeros(acc.shape, F32)
    ins[0].wait()
    outs = []
    for h in range(2):
        ins[1 + h].wait()

        def add(s, carry):
            for i in range(4):
                for k in range(2):
                    at = got[s * 4 + i, 0, k * NB + me]
                    acc[h, at] += arr[h, s * 4 + i, k]
            return carry

        lax.fori_loop(0, NB // 4, add, 0)
        if h == 0:
            ins[3].wait()
            outs.append(pltpu.make_async_copy(vel, velo_ref, sem.at[4]))
            outs[0].start()
        for q in range(2):
            for c in range(2):
                lanes = slice((h * 2 + c) * LANE, (h * 2 + c + 1) * LANE)
                for b in range(NB):
                    out[q, b * BR : b * BR + BR, lanes] = acc[
                        h, b, q * 8 + c * BR : q * 8 + c * BR + BR, :
                    ]
    for q, ref in enumerate((mass_ref, heat_ref)):
        outs.append(pltpu.make_async_copy(out.at[q], ref, sem.at[5 + q]))
        outs[-1].start()
    for copy in outs:
        copy.wait()


def shards(state, order, sweep, owner, slot_target):
    any_ = pl.BlockSpec(memory_space=pl.ANY)
    vmem = pl.BlockSpec(memory_space=pltpu.VMEM)
    smem = pl.BlockSpec(memory_space=pltpu.SMEM)
    dma = pltpu.SemaphoreType.DMA
    half = jax.ShapeDtypeStruct((NB, 2, 16, LANE), F32)
    arr_a, arr_b, got, vel = pl.pallas_call(
        main_kernel,
        name="step",
        out_shape=(
            half,
            half,
            jax.ShapeDtypeStruct((NB, 1, LANE), jnp.int32),
            jax.ShapeDtypeStruct((2, ROWS, W), F32),
        ),
        in_specs=[smem, vmem, vmem, any_, vmem],
        out_specs=(any_, any_, any_, any_),
        scratch_shapes=[
            pltpu.VMEM((5, ROWS, W), F32),
            pltpu.VMEM((NB, 5, EARLY, BR, LANE), F32),
            pltpu.VMEM((NB, 5, LATE, BR, LANE), F32),
            pltpu.VMEM((NB, 5, EARLY, BR, LANE), F32),
            pltpu.VMEM((NB, 5, LATE, BR, LANE), F32),
            pltpu.VMEM((NB, 5, EARLY, BR, LANE), F32),
            pltpu.VMEM((NB, 5, LATE, BR, LANE), F32),
            pltpu.VMEM((2, 5, EARLY, BR, LANE), F32),
            pltpu.VMEM((2, 5, LATE, BR, LANE), F32),
            pltpu.VMEM((5, PIECES, EXT, LANE), F32),
            pltpu.VMEM((5, PIECES, EXT, LANE), F32),
            pltpu.VMEM((PIECES, EXT, LANE), F32),
            pltpu.VMEM((PIECES, EXT, LANE), F32),
            pltpu.VMEM((NB, 16, LANE), F32),
            pltpu.VMEM((NB, 16, LANE), F32),
            pltpu.VMEM((NB, 2, 16, LANE), F32),
            pltpu.VMEM((NB, 2, 16, LANE), F32),
            pltpu.VMEM((2, ROWS, W), F32),
            pltpu.VMEM((1, LANE), jnp.int32),
            pltpu.SMEM((1, LANE), jnp.int32),
            dma((5,)),
            dma((NB,)), dma((NB,)), dma((NB,)), dma((NB,)),
            dma((NB,)), dma((NB,)),
            dma((4,)), dma((4,)),
            dma((NB,)), dma((NB,)), dma((NB,)), dma((NB,)),
            dma((5,)),
        ],
        compiler_params=pltpu.CompilerParams(collective_id=0, has_side_effects=True),
    )(order, owner.reshape(1, NB), slot_target.reshape(1, NB), state, sweep)
    field = jax.ShapeDtypeStruct((ROWS, W), F32)
    return pl.pallas_call(
        last_kernel,
        name="gather",
        out_shape=(field, field, jax.ShapeDtypeStruct((2, ROWS, W), F32)),
        in_specs=[any_, any_, any_, any_],
        out_specs=(any_, any_, any_),
        scratch_shapes=[
            pltpu.SMEM((NB, 1, LANE), jnp.int32),
            pltpu.VMEM((2, NB, 2, 16, LANE), F32),
            pltpu.VMEM((2, ROWS, W), F32),
            pltpu.VMEM((2, NB + 1, 16, LANE), F32),
            pltpu.VMEM((2, ROWS, W), F32),
            dma((7,)),
        ],
    )(got, arr_a, arr_b, vel)


def solution(mesh):
    rows = P(("grp", "bis"), None)
    return jax.shard_map(
        shards,
        mesh=mesh,
        in_specs=(P(None, ("grp", "bis"), None), rows, rows, rows, P(("grp", "bis"))),
        out_specs=(rows, rows, P(None, ("grp", "bis"), None)),
        check_vma=False,
    )
```

time: 165 us -> 47.5 us (0.29); the launches traced: 163 us -> 47.3 us
  waiting for transfers between devices: 75.3 us -> 0 us
  Pallas kernels: 0 us -> 46.7 us
  starting transfers between devices: 38.4 us -> 0 us
  local copies, waits for them, and re-layouts: 27.9 us -> 0 us
  other arithmetic: 18.3 us -> 0 us
    ppermute x9 -> x0, waiting for transfers between devices: 60.6 us -> none  [the longest x5 60.6 us: from_partner(): return lax.ppermute(block, axis, route)]
    pallas_call x0 -> x2, Pallas kernels: none -> 46.7 us  [the longest x1 44.1 us: shards(): pl.pallas_call(main_kernel, name='step', out_shape=(half, half, jax.Shape...]
    ppermute x9 -> x0, starting transfers between devices: 20.3 us -> none  [the longest x2 7.76 us: with_halo(): lax.ppermute(lax.slice_in_dim(block, 0, width, axis=dim), axis, backward)]
    all_to_all x2 -> x0, starting transfers between devices: 18.1 us -> none  [the longest x1 10.6 us: shards(): lax.all_to_all(labels.reshape(1, nbis, CAP), 'bis', split_axis=1, concat_...]
    all_to_all x2 -> x0, waiting for transfers between devices: 14.7 us -> none  [the longest x1 14.7 us: shards(): lax.all_to_all(outgoing.reshape(2, nbis, CAP * flat), 'bis', split_axis=1...]
    another operation x12 -> x0, other arithmetic: 8.09 us -> none  [the longest x8 4.5 us: shards(): moved = jnp.stack([lower, upper], axis=2).reshape(5, nbis, flat)]
    select_n x8 -> x0, other arithmetic: 6.43 us -> none  [the longest x2 2.83 us: shards(): picked = jnp.take(state.reshape(5, nbis, flat), order[0], axis=1)]
    slice x11 -> x0, local copies, waits for them, and re-layouts: 6.14 us -> none  [the longest x1 1.82 us: advance(): ene[1:-1] * (1.0 - STEP_DT * (center_g - 1.0) * spread)]
  transfers between devices with their start and end apart: 11 -> 0, of which waited for: 6 -> 0; matrix products, arithmetic and copies ran while one was open for 10% -> 0% of each run, Pallas kernels for 0% -> 0%
where the time goes in v2:
time: 47.5 us; the launch traced here: 47.3 us
  Pallas kernels  46.7 us (98%)
  between operations  0.64 us (1%)
    pallas_call x1, Pallas kernels, shards(): pl.pallas_call(main_kernel, name='step', out_shape=(half, half, jax.Shape...  44.1 us
    pallas_call x1, Pallas kernels, shards(): pl.pallas_call(last_kernel, name='gather', out_shape=(field, field, jax.S...  2.6 us

profile of v2, /device:TPU:1, one launch (start us, length us, event | category | flops | bytes accessed | tf_op | source)
XLA Modules:
  0.0 47.3 jit_solution(15180442978720239245)
XLA Ops:
  0.6 44.1 %step.1 = (f32[32,2,16,128]{3,2,1,0:T(8,128)}, f32[32,2,16,128]{3,2,1,0:T(8,128)}, s32[32,1,128]{2,1,0:T(1,128)}, f32[2,128,512]{2,1,0:T(8,128)}) custom-call(s32[1,32]{1,0:T(1,128)} %order_ref.1, s32[1,32]{1,0:T(1,128)} %bitcast.2, s32[1,32]{1,0:T(1,128)} %bitcast.3, f32[5,128,512]{2,1,0:T(8,128)} %state_ref.1, f32[128,512]{1,0:T(8,128)} %sweep_ref.1), custom_call_target="tpu_custom_call" | custom-call | tf_op jit(solution)/shard_map/step/pallas_call | solution.py:454
  44.8 2.6 %gather.1 = (f32[128,512]{1,0:T(8,128)}, f32[128,512]{1,0:T(8,128)}, f32[2,128,512]{2,1,0:T(8,128)}) custom-call(s32[32,1,128]{2,1,0:T(1,128)} %get-tuple-element.7.got_ref, f32[32,2,16,128]{3,2,1,0:T(8,128)} %get-tuple-element.8.arr_a, f32[32,2,16,128]{3,2,1,0:T(8,128)} %get-tuple-element.9.arr_b, f32[2,128,512]{2,1,0:T(8,128)} %get-tuple-element.10.vel_ref), custom_call_target="tpu_custom_call" | custom-call | tf_op jit(solution)/shard_map/gather/pallas_call | solution.py:496

commit v3 on v2

--- a/solution.py
+++ b/solution.py
@@ -18,16 +18,13 @@
 TOP = 16
 EXT = TOP + ROWS + 16
 MESH = pl.DeviceIdType.MESH
-STRIDE = 13
-HOLD = 16
+STRIDE = 9
+HALF = BR // 2
+PAIRS = NB // 2
 F32 = jnp.float32
 
 
-def neighbour(me, k):
-    j = lax.rem(k * STRIDE, NB)
-    x, y, c = me // 8, lax.rem(me // 2, 4), lax.rem(me, 2)
-    dx, dy, dc = j // 8, lax.rem(j // 2, 4), lax.rem(j, 2)
-    return lax.rem(x + dx, 4) * 8 + lax.rem(y + dy, 4) * 2 + lax.rem(c + dc, 2)
+ORDER = [(j // 8, j // 2 % 4, j % 2) for j in (k * STRIDE % NB for k in range(1, NB))]
 
 
 def lane_mask(size, lane):
@@ -67,9 +64,9 @@
 def main_kernel(
     order_ref, owner_ref, slot_ref, state_ref, sweep_ref,
     arr_a, arr_b, got_ref, vel_ref,
-    xv, lin_a, lin_b, snd_a, snd_b, msg_a, msg_b, hal_a, hal_b,
+    xv, lin_a, lin_b, snd_a, snd_b, msg_a, msg_b, dir_a, dir_b, hal_a, hal_b, fwd_a, fwd_b,
     ext, one, press0, press1, part_a, part_b, out_a, out_b, vel, plan_v, plan_s,
-    in_sem, s1a, r1a, s1b, r1b, sm, rm, sh, rh, s2a, r2a, s2b, r2b, loc,
+    in_sem, s1a, r1a, s1b, r1b, sm, rm, sd, sh, rh, s2a, r2a, s2b, r2b, loc,
 ):
     grp = lax.axis_index("grp")
     me = lax.axis_index("bis")
@@ -80,6 +77,18 @@
     last_one = me == NB - 1
     low = (grp - first_one.astype(jnp.int32), lax.rem(me + NB - 1, NB))
     high = (grp + last_one.astype(jnp.int32), lax.rem(me + 1, NB))
+    odd = lax.rem(me, 2)
+    at_x = [lax.rem(me // 8 + d, 4) * 8 for d in range(4)]
+    at_y = [lax.rem(me // 2 + d, 4) * 2 for d in range(4)]
+    at_c = [odd, 1 - odd]
+    peers = [at_x[dx] + at_y[dy] + at_c[dc] for dx, dy, dc in ORDER]
+    odd_not = 1 - odd
+    partner = me + 1 - 2 * odd
+    inside = (NB - 1) * odd_not
+    has_direct = jnp.where(odd == 0, has_low, has_high)
+    sends_direct = jnp.logical_or(first_one, last_one)
+    begin = jnp.logical_and(first_one, grp == 0).astype(jnp.int32)
+    end = PAIRS - jnp.logical_and(last_one, grp == NG - 1).astype(jnp.int32)
     far_low = jnp.logical_and(first_one, has_low)
     far_high = jnp.logical_and(last_one, has_high)
 
@@ -89,19 +98,28 @@
 
     barrier = pltpu.get_barrier_semaphore()
 
-    def loop(lo, hi, body):
+    def loop(lo, hi, body, unroll=1):
         def step(k, carry):
             body(k)
             return carry
 
-        lax.fori_loop(lo, hi, step, 0)
-
-    def greet(k):
-        pl.semaphore_signal(
-            barrier, inc=1, device_id=(grp, neighbour(me, k)), device_id_type=MESH
+        lax.fori_loop(lo, hi, step, 0, unroll=unroll)
+
+    def others(body):
+        def step(d, carry):
+            @pl.when(d != me)
+            def _():
+                body(d)
+
+            return carry
+
+        lax.fori_loop(0, NB, step, 0)
+
+    others(
+        lambda d: pl.semaphore_signal(
+            barrier, inc=1, device_id=(grp, d), device_id_type=MESH
         )
-
-    loop(1, NB, greet)
+    )
 
     @pl.when(far_low)
     def _():
@@ -177,27 +195,51 @@
     def share_b(d, source):
         return remote(out_b.at[d], arr_b.at[source], s2b.at[d], r2b.at[source], d)
 
-    def fill_a(k):
-        d = neighbour(me, k)
+    def direct_one(dire, hal, j, at):
+        index = 2 * j + 3 * odd - 1
+        step = (index + NB) // NB - 1
+        return pltpu.make_async_remote_copy(
+            src_ref=dire.at[j], dst_ref=hal, send_sem=sd.at[at, j], recv_sem=rh.at[2 + at],
+            device_id=(grp + step, index - step * NB), device_id_type=MESH,
+        )
+
+    def direct(dire, hal, lin, at):
+        @pl.when(first_one)
+        def _():
+            def pack(j):
+                dire[j] = lin[order_ref[0, 2 * j], :, :, 0:HALF]
+
+            loop(begin, end, pack)
+
+        @pl.when(last_one)
+        def _():
+            def pack(j):
+                dire[j] = lin[order_ref[0, 2 * j + 1], :, :, HALF:BR]
+
+            loop(begin, end, pack)
+
+        @pl.when(sends_direct)
+        def _():
+            loop(begin, end, lambda j: direct_one(dire, hal, j, at).start())
+
+    def fill_a(d):
         snd_a[d] = lin_a[order_ref[0, d]]
 
-    def fill_b(k):
-        d = neighbour(me, k)
+    def fill_b(d):
         snd_b[d] = lin_b[order_ref[0, d]]
 
-    fill_a(1)
-
-    def go_a(k):
-        @pl.when(k < NB - 1)
-        def _():
-            fill_a(k + 1)
-
-        move_a(neighbour(me, k), me).start()
-
-    loop(1, NB, go_a)
-    loop(1, NB, fill_b)
-    loop(1, NB - HOLD, lambda k: move_b(neighbour(me, k), me).start())
-    loop(1, NB, lambda k: tell(neighbour(me, k), me).start())
+    def rounds(fill, send):
+        fill(peers[0])
+        for k, d in enumerate(peers):
+            if k + 1 < len(peers):
+                fill(peers[k + 1])
+            send(d, me).start()
+
+    rounds(fill_a, move_a)
+    direct(dir_a, hal_a, lin_a, 0)
+    rounds(fill_b, move_b)
+    direct(dir_b, hal_b, lin_b, 1)
+    others(lambda d: tell(d, me).start())
     own_plan = pltpu.make_async_copy(plan_v, got_ref.at[me], loc.at[1])
     own_plan.start()
     msg_a[me] = lin_a[order_ref[0, me]]
@@ -211,72 +253,44 @@
         press0[c, 0:TOP, :] = zero
         press0[c, EXT - 16 : EXT, :] = zero
 
-    def spread_out(values, c, at):
+    def spread_out(values, c, at, size=BR):
         for f in range(5):
-            ext[f, c, pl.ds(at, BR), :] = values[f]
-        press0[c, pl.ds(at, BR), :] = (values[4] - 1.0) * values[0] * values[1]
+            ext[f, c, pl.ds(at, size), :] = values[f]
+        press0[c, pl.ds(at, size), :] = (values[4] - 1.0) * values[0] * values[1]
 
     def unpack(msg, base, count, source):
         for c in range(count):
             spread_out([msg[source, f, c] for f in range(5)], base + c, TOP + source * BR)
 
-    def halo(hal, msg, at):
-        up = pltpu.make_async_remote_copy(
-            src_ref=msg.at[NB - 1], dst_ref=hal.at[0], send_sem=sh.at[at], recv_sem=rh.at[at],
-            device_id=high, device_id_type=MESH,
-        )
-        down = pltpu.make_async_remote_copy(
-            src_ref=msg.at[0], dst_ref=hal.at[1], send_sem=sh.at[at + 1], recv_sem=rh.at[at + 1],
-            device_id=low, device_id_type=MESH,
-        )
-        return up, down
-
-    def pass_on(pair, move):
-        up, down = pair
-
-        @pl.when(jnp.logical_not(last_one))
-        def _():
-            move(NB - 1, NB - 1).wait_recv()
-
-        @pl.when(has_high)
-        def _():
-            up.start()
-
-        @pl.when(jnp.logical_not(first_one))
-        def _():
-            move(0, 0).wait_recv()
-
-        @pl.when(has_low)
-        def _():
-            down.start()
+    def forward(msg, fwd, at):
+        return remote(msg.at[inside], fwd, sh.at[at], rh.at[at], partner)
+
+    def pass_on(msg, fwd, move, at):
+        move(inside, inside).wait_recv()
+        forward(msg, fwd, at).start()
 
     def collect(move, msg, base, count):
-        def one_source(k):
-            source = neighbour(me, k)
-
-            @pl.when(jnp.logical_and(source > 0, source < NB - 1))
+        def one_source(source):
+            @pl.when(jnp.logical_and(source != inside, source != me))
             def _():
                 move(source, source).wait_recv()
 
             unpack(msg, base, count, source)
 
-        loop(1, NB, one_source)
-        unpack(msg, base, count, me)
-
-    def halo_in(pair, hal, base, count):
-        up, down = pair
-
-        @pl.when(has_low)
+        loop(0, NB, one_source)
+
+    def halo_in(dire, hal, msg, fwd, base, count, at):
+        forward(msg, fwd, at).wait_recv()
+        beside = TOP - BR + odd_not * (ROWS + BR)
+        for c in range(count):
+            spread_out([fwd[f, c] for f in range(5)], base + c, beside)
+
+        @pl.when(has_direct)
         def _():
-            up.wait_recv()
+            direct_one(dire, hal, 0, at).wait_recv()
+            across = TOP - HALF + odd * (ROWS + HALF)
             for c in range(count):
-                spread_out([hal[0, f, c] for f in range(5)], base + c, TOP - BR)
-
-        @pl.when(has_high)
-        def _():
-            down.wait_recv()
-            for c in range(count):
-                spread_out([hal[1, f, c] for f in range(5)], base + c, TOP + ROWS)
+                spread_out([hal[f, c] for f in range(5)], base + c, across, HALF)
 
     start = [ext.at[f] for f in range(5)]
     after = [one.at[f] for f in range(4)] + [ext.at[4]]
@@ -322,8 +336,8 @@
                     part[block + i, put : put + BR, :] = value[i * BR : i * BR + BR]
 
     def inner_rows(pieces, closed, results, part):
-        loop(0, 7, lambda i: first(pieces, pl.multiple_of(TOP + 8 + i * 16, 8), 16, closed))
-        loop(0, 6, lambda i: second(results, 4 + i * 4, 16, part))
+        loop(0, 7, lambda i: first(pieces, pl.multiple_of(TOP + 8 + i * 16, 8), 16, closed), 7)
+        loop(0, 6, lambda i: second(results, 4 + i * 4, 16, part), 3)
 
     def edge_rows(pieces, closed, results, part):
         first(pieces, TOP - 8, 8, closed, has_low)
@@ -331,15 +345,11 @@
         loop(0, 2, lambda j: first(pieces, pl.multiple_of(TOP + j * (ROWS - 8), 8), 8, closed))
         loop(0, 2, lambda j: second(results, j * (NB - 4), 16, part))
 
-    pair_a = halo(hal_a, msg_a, 0)
-    pair_b = halo(hal_b, msg_b, 2)
-
-    pass_on(pair_a, move_a)
-    loop(NB - HOLD, NB, lambda k: move_b(neighbour(me, k), me).start())
+    pass_on(msg_a, fwd_a, move_a, 0)
     collect(move_a, msg_a, 0, EARLY)
     early, late = (0, 1), (2, 3)
     inner_rows((0, 1, 2), 2, early, part_a)
-    halo_in(pair_a, hal_a, 0, EARLY)
+    halo_in(dir_a, hal_a, msg_a, fwd_a, 0, EARLY, 0)
     edge_rows((0, 1, 2), 2, early, part_a)
 
     plan_copy.wait()
@@ -348,26 +358,24 @@
         out[d, 0] = part[plan_s[0, 2 * NB + d]]
         out[d, 1] = part[plan_s[0, 3 * NB + d]]
 
-    loop(0, NB, lambda d: fill2(out_a, part_a, d))
-    loop(1, NB - HOLD, lambda k: share_a(neighbour(me, k), me).start())
+    rounds(lambda d: fill2(out_a, part_a, d), share_a)
+    fill2(out_a, part_a, me)
     own_a = pltpu.make_async_copy(out_a.at[me], arr_a.at[me], loc.at[2])
     own_a.start()
 
-    pass_on(pair_b, move_b)
-    loop(NB - HOLD, NB, lambda k: share_a(neighbour(me, k), me).start())
+    pass_on(msg_b, fwd_b, move_b, 1)
     collect(move_b, msg_b, EARLY, LATE)
     inner_rows((2, 3), None, late, part_b)
-    halo_in(pair_b, hal_b, EARLY, LATE)
+    halo_in(dir_b, hal_b, msg_b, fwd_b, EARLY, LATE, 1)
     edge_rows((2, 3), None, late, part_b)
-    loop(0, NB, lambda d: fill2(out_b, part_b, d))
-    loop(1, NB, lambda k: share_b(neighbour(me, k), me).start())
+    rounds(lambda d: fill2(out_b, part_b, d), share_b)
+    fill2(out_b, part_b, me)
     own_b = pltpu.make_async_copy(out_b.at[me], arr_b.at[me], loc.at[3])
     own_b.start()
     vel_out = pltpu.make_async_copy(vel, vel_ref, loc.at[4])
     vel_out.start()
 
-    def finish(k):
-        d = neighbour(me, k)
+    def finish(d):
         move_a(d, me).wait_send()
         move_b(d, me).wait_send()
         tell(d, me).wait_send()
@@ -375,29 +383,26 @@
         share_a(d, me).wait_send()
         share_a(d, d).wait_recv()
 
-    loop(1, NB, finish)
-
-    @pl.when(has_high)
+    others(finish)
+
+    forward(msg_a, fwd_a, 0).wait_send()
+    forward(msg_b, fwd_b, 1).wait_send()
+
+    @pl.when(sends_direct)
     def _():
-        pair_a[0].wait_send()
-        pair_b[0].wait_send()
-
-    @pl.when(has_low)
-    def _():
-        pair_a[1].wait_send()
-        pair_b[1].wait_send()
+        for at, (dire, hal) in enumerate(((dir_a, hal_a), (dir_b, hal_b))):
+            loop(begin, end, lambda j, a=(dire, hal), at=at: direct_one(*a, j, at).wait_send())
 
     own_plan.wait()
     own_a.wait()
     own_b.wait()
     vel_out.wait()
 
-    def finish_b(k):
-        d = neighbour(me, k)
+    def finish_b(d):
         share_b(d, me).wait_send()
         share_b(d, d).wait_recv()
 
-    loop(1, NB, finish_b)
+    others(finish_b)
 
 
 def last_kernel(
@@ -470,8 +475,12 @@
             pltpu.VMEM((NB, 5, LATE, BR, LANE), F32),
             pltpu.VMEM((NB, 5, EARLY, BR, LANE), F32),
             pltpu.VMEM((NB, 5, LATE, BR, LANE), F32),
-            pltpu.VMEM((2, 5, EARLY, BR, LANE), F32),
-            pltpu.VMEM((2, 5, LATE, BR, LANE), F32),
+            pltpu.VMEM((PAIRS, 5, EARLY, HALF, LANE), F32),
+            pltpu.VMEM((PAIRS, 5, LATE, HALF, LANE), F32),
+            pltpu.VMEM((5, EARLY, HALF, LANE), F32),
+            pltpu.VMEM((5, LATE, HALF, LANE), F32),
+            pltpu.VMEM((5, EARLY, BR, LANE), F32),
+            pltpu.VMEM((5, LATE, BR, LANE), F32),
             pltpu.VMEM((5, PIECES, EXT, LANE), F32),
             pltpu.VMEM((5, PIECES, EXT, LANE), F32),
             pltpu.VMEM((PIECES, EXT, LANE), F32),
@@ -486,7 +495,7 @@
             dma((5,)),
             dma((NB,)), dma((NB,)), dma((NB,)), dma((NB,)),
             dma((NB,)), dma((NB,)),
-            dma((4,)), dma((4,)),
+            dma((2, PAIRS)), dma((2,)), dma((4,)),
             dma((NB,)), dma((NB,)), dma((NB,)), dma((NB,)),
             dma((5,)),
         ],

time: 47.5 us -> 45.2 us (0.952)
  Pallas kernels: 46.7 us -> 44.1 us
    pallas_call x1, Pallas kernels: 44.1 us -> 41.5 us  [shards(): pl.pallas_call(main_kernel, name='step', out_shape=(half, half, jax.Shape...]
where the time goes in v3:
time: 45.2 us; the launch traced here: 44.7 us
  Pallas kernels  44.1 us (98%)
  between operations  0.64 us (1%)
    pallas_call x1, Pallas kernels, shards(): pl.pallas_call(main_kernel, name='step', out_shape=(half, half, jax.Shape...  41.5 us
    pallas_call x1, Pallas kernels, shards(): pl.pallas_call(last_kernel, name='gather', out_shape=(field, field, jax.S...  2.59 us

profile of v3, /device:TPU:1, one launch (start us, length us, event | category | flops | bytes accessed | tf_op | source)
XLA Modules:
  0.0 44.7 jit_solution(14431840329879706641)
XLA Ops:
  0.6 41.5 %step.1 = (f32[32,2,16,128]{3,2,1,0:T(8,128)}, f32[32,2,16,128]{3,2,1,0:T(8,128)}, s32[32,1,128]{2,1,0:T(1,128)}, f32[2,128,512]{2,1,0:T(8,128)}) custom-call(s32[1,32]{1,0:T(1,128)} %order_ref.1, s32[1,32]{1,0:T(1,128)} %bitcast.2, s32[1,32]{1,0:T(1,128)} %bitcast.3, f32[5,128,512]{2,1,0:T(8,128)} %state_ref.1, f32[128,512]{1,0:T(8,128)} %sweep_ref.1), custom_call_target="tpu_custom_call" | custom-call | tf_op jit(solution)/shard_map/step/pallas_call | solution.py:459
  42.1 2.6 %gather.1 = (f32[128,512]{1,0:T(8,128)}, f32[128,512]{1,0:T(8,128)}, f32[2,128,512]{2,1,0:T(8,128)}) custom-call(s32[32,1,128]{2,1,0:T(1,128)} %get-tuple-element.7.got_ref, f32[32,2,16,128]{3,2,1,0:T(8,128)} %get-tuple-element.8.arr_a, f32[32,2,16,128]{3,2,1,0:T(8,128)} %get-tuple-element.9.arr_b, f32[2,128,512]{2,1,0:T(8,128)} %get-tuple-element.10.vel_ref), custom_call_target="tpu_custom_call" | custom-call | tf_op jit(solution)/shard_map/gather/pallas_call | solution.py:505
